TPU v7x, 32 devices: a whole 2x2x4 slice. The times are simulated.
32 devices in a mesh: dp: 2 (over x), col: 4 (over z), row: 4 (over y, core).
Axes of the slice: x: 2, y: 2, z: 4, core: 2. Of those that a mesh axis runs over, the one named last changes fastest.
Arguments:
- seq_in: bfloat16 [16, 128, 5760], P(None, 'dp', 'row'), parts along dimension 1
- w_in1: bfloat16 [5760, 23040], P('row', 'col')
- w_rec1: bfloat16 [5760, 23040], P('row', 'col')
- b_gate1: float32 [23040], P(('col', 'row'))
- w_in2: bfloat16 [5760, 23040], P('row', 'col')
- w_rec2: bfloat16 [5760, 23040], P('row', 'col')
- b_gate2: float32 [23040], P(('col', 'row'))
- h_init: float32 [2, 128, 5760], P(None, 'dp', 'row'), parts along dimension 1
- c_init: float32 [2, 128, 5760], P(None, 'dp', 'row'), parts along dimension 1
Outputs:
- output 1: bfloat16 [16, 128, 5760], P(None, 'dp', ('row', 'col')), parts along dimension 1
- output 2: float32 [128, 5760], P('dp', ('row', 'col')), parts along dimension 0
- output 3: float32 [128, 5760], P('dp', ('row', 'col')), parts along dimension 0
There are 2 independent parts. A program takes and returns all parts, laid end to end along the dimension named above; an argument that names none is the same for every part.
All inputs are finite; a program needn't handle non-finite values.
Results may differ from a plain program's by a relative error of at most 0.00285702.
Values are sent between devices in bfloat16 or wider.
A program may use at most 1 GiB of HBM per device.

v0:
```python
import jax
import jax.numpy as jnp
from jax import lax
from jax.sharding import PartitionSpec as P


def gate_update(z_own, c_prev):
    unit_dev = c_prev.shape[-1]
    in_gate = jax.nn.sigmoid(z_own[:, :unit_dev])
    forget = jax.nn.sigmoid(z_own[:, unit_dev:2 * unit_dev])
    cell_in = jnp.tanh(z_own[:, 2 * unit_dev:3 * unit_dev])
    out_gate = jax.nn.sigmoid(z_own[:, 3 * unit_dev:])
    c_new = forget * c_prev + in_gate * cell_in
    h_new = (out_gate * jnp.tanh(c_new)).astype(jnp.bfloat16)
    return h_new, c_new


def solution(mesh):
    def lstm_layer(in_rows, w_in, w_rec, b_own, h_rows, c_own, keep_rows):
        def lstm_step(carry_in, in_step):
            h_prev, c_prev = carry_in
            part_sum = jnp.dot(in_step, w_in, preferred_element_type=jnp.float32)
            part_sum = part_sum + jnp.dot(h_prev, w_rec, preferred_element_type=jnp.float32)
            z_own = lax.psum_scatter(part_sum, "row", scatter_dimension=1, tiled=True) + b_own
            h_own, c_new = gate_update(z_own, c_prev)
            h_next = lax.all_gather(h_own, "col", axis=1, tiled=True)
            return (h_next, c_new), (h_next if keep_rows else h_own)

        return lax.scan(lstm_step, (h_rows, c_own), in_rows)

    def local_program(seq_in, w_in1, w_rec1, b_gate1, w_in2, w_rec2, b_gate2, h_init, c_init):
        unit_dev = b_gate1.shape[0] // 4
        col_index = lax.axis_index("col")

        def own_cells(layer_idx):
            return lax.dynamic_slice_in_dim(c_init[layer_idx], col_index * unit_dev, unit_dev, axis=1)

        carry_one, h1_rows = lstm_layer(seq_in, w_in1, w_rec1, b_gate1, h_init[0].astype(jnp.bfloat16), own_cells(0), True)
        carry_two, h2_own = lstm_layer(h1_rows, w_in2, w_rec2, b_gate2, h_init[1].astype(jnp.bfloat16), own_cells(1), False)
        return h2_own, carry_one[1], carry_two[1]

    row_spec = P(None, "dp", "row")
    weight_spec = P("row", "col")
    bias_spec = P(("col", "row"))
    seq_out_spec = P(None, "dp", ("row", "col"))
    cell_out_spec = P("dp", ("row", "col"))
    return jax.shard_map(
        local_program,
        mesh=mesh,
        in_specs=(row_spec, weight_spec, weight_spec, bias_spec, weight_spec, weight_spec, bias_spec, row_spec, row_spec),
        out_specs=(seq_out_spec, cell_out_spec, cell_out_spec),
        check_vma=False,
    )
```

profile of v0, /device:TPU:0, one launch (start us, length us, event | category | flops | bytes accessed | tf_op | source)
XLA Modules:
  0.0 2227.4 jit_solution(3049768171077893734)
XLA Ops:
  9.7 1106.4 %while.28 = (s32[]{:T(128)}, bf16[64,1440]{1,0:T(8,128)(2,1)S(1)}, f32[64,360]{1,0:T(8,128)S(1)}, bf16[16,64,1440]{2,1,0:T(8,128)(2,1)}, bf16[16,64,1440]{2,1,0:...) while((s32[]{:T(128)}, bf16[64,1440]{1,0:T(8,128)(2,1)S(1)}, ...), condition=%wide.region_2.3_spmd, body=%wide.region_0.2_spmd.sunk | while | flops 2124149760 | bytes 118087472 | solution.py:29
  25.7 39.2 %reduce-scatter.11.cloned.1.call-done = f32[1440,64]{1,0:T(8,128)} async-done(((f32[5760,64]{1,0:T(8,128)}), f32[1440,64]{1,0:T(8,128)}) %reduce-scatter.11.cloned.1.call-update) | async-done | bytes 368656 | tf_op jit(solution)/shard_map/while
  97.0 36.9 %reduce-scatter.11.cloned.1.call-done = f32[1440,64]{1,0:T(8,128)} async-done(((f32[5760,64]{1,0:T(8,128)}), f32[1440,64]{1,0:T(8,128)}) %reduce-scatter.11.cloned.1.call-update) | async-done | bytes 368656 | tf_op jit(solution)/shard_map/while
  235.0 36.9 %reduce-scatter.11.cloned.1.call-done = f32[1440,64]{1,0:T(8,128)} async-done(((f32[5760,64]{1,0:T(8,128)}), f32[1440,64]{1,0:T(8,128)}) %reduce-scatter.11.cloned.1.call-update) | async-done | bytes 368656 | tf_op jit(solution)/shard_map/while
  304.0 36.8 %reduce-scatter.11.cloned.1.call-done = f32[1440,64]{1,0:T(8,128)} async-done(((f32[5760,64]{1,0:T(8,128)}), f32[1440,64]{1,0:T(8,128)}) %reduce-scatter.11.cloned.1.call-update) | async-done | bytes 368656 | tf_op jit(solution)/shard_map/while
  373.0 36.9 %reduce-scatter.11.cloned.1.call-done = f32[1440,64]{1,0:T(8,128)} async-done(((f32[5760,64]{1,0:T(8,128)}), f32[1440,64]{1,0:T(8,128)}) %reduce-scatter.11.cloned.1.call-update) | async-done | bytes 368656 | tf_op jit(solution)/shard_map/while
  442.0 36.9 %reduce-scatter.11.cloned.1.call-done = f32[1440,64]{1,0:T(8,128)} async-done(((f32[5760,64]{1,0:T(8,128)}), f32[1440,64]{1,0:T(8,128)}) %reduce-scatter.11.cloned.1.call-update) | async-done | bytes 368656 | tf_op jit(solution)/shard_map/while
  511.0 36.9 %reduce-scatter.11.cloned.1.call-done = f32[1440,64]{1,0:T(8,128)} async-done(((f32[5760,64]{1,0:T(8,128)}), f32[1440,64]{1,0:T(8,128)}) %reduce-scatter.11.cloned.1.call-update) | async-done | bytes 368656 | tf_op jit(solution)/shard_map/while
  580.0 36.9 %reduce-scatter.11.cloned.1.call-done = f32[1440,64]{1,0:T(8,128)} async-done(((f32[5760,64]{1,0:T(8,128)}), f32[1440,64]{1,0:T(8,128)}) %reduce-scatter.11.cloned.1.call-update) | async-done | bytes 368656 | tf_op jit(solution)/shard_map/while
  649.0 36.9 %reduce-scatter.11.cloned.1.call-done = f32[1440,64]{1,0:T(8,128)} async-done(((f32[5760,64]{1,0:T(8,128)}), f32[1440,64]{1,0:T(8,128)}) %reduce-scatter.11.cloned.1.call-update) | async-done | bytes 368656 | tf_op jit(solution)/shard_map/while
  718.0 36.9 %reduce-scatter.11.cloned.1.call-done = f32[1440,64]{1,0:T(8,128)} async-done(((f32[5760,64]{1,0:T(8,128)}), f32[1440,64]{1,0:T(8,128)}) %reduce-scatter.11.cloned.1.call-update) | async-done | bytes 368656 | tf_op jit(solution)/shard_map/while
  787.0 36.9 %reduce-scatter.11.cloned.1.call-done = f32[1440,64]{1,0:T(8,128)} async-done(((f32[5760,64]{1,0:T(8,128)}), f32[1440,64]{1,0:T(8,128)}) %reduce-scatter.11.cloned.1.call-update) | async-done | bytes 368656 | tf_op jit(solution)/shard_map/while
  856.0 36.8 %reduce-scatter.11.cloned.1.call-done = f32[1440,64]{1,0:T(8,128)} async-done(((f32[5760,64]{1,0:T(8,128)}), f32[1440,64]{1,0:T(8,128)}) %reduce-scatter.11.cloned.1.call-update) | async-done | bytes 368656 | tf_op jit(solution)/shard_map/while
  924.9 36.9 %reduce-scatter.11.cloned.1.call-done = f32[1440,64]{1,0:T(8,128)} async-done(((f32[5760,64]{1,0:T(8,128)}), f32[1440,64]{1,0:T(8,128)}) %reduce-scatter.11.cloned.1.call-update) | async-done | bytes 368656 | tf_op jit(solution)/shard_map/while
  994.0 36.8 %reduce-scatter.11.cloned.1.call-done = f32[1440,64]{1,0:T(8,128)} async-done(((f32[5760,64]{1,0:T(8,128)}), f32[1440,64]{1,0:T(8,128)}) %reduce-scatter.11.cloned.1.call-update) | async-done | bytes 368656 | tf_op jit(solution)/shard_map/while
  1062.9 36.9 %reduce-scatter.11.cloned.1.call-done = f32[1440,64]{1,0:T(8,128)} async-done(((f32[5760,64]{1,0:T(8,128)}), f32[1440,64]{1,0:T(8,128)}) %reduce-scatter.11.cloned.1.call-update) | async-done | bytes 368656 | tf_op jit(solution)/shard_map/while
  1116.7 1103.5 %while.29 = (s32[]{:T(128)}, bf16[64,1440]{1,0:T(8,128)(2,1)S(1)}, f32[64,360]{1,0:T(8,128)S(1)}, bf16[16,64,360]{2,1,0:T(8,128)(2,1)}, bf16[16,64,1440]{2,1,0:T...) while((s32[]{:T(128)}, bf16[64,1440]{1,0:T(8,128)(2,1)S(1)}, ...), condition=%wide.region_5.6_spmd, body=%wide.region_3.5_spmd.sunk | while | flops 2124149760 | bytes 117755696 | solution.py:29
  1201.6 36.9 %reduce-scatter.13.cloned.1.call-done = f32[1440,64]{1,0:T(8,128)} async-done(((f32[5760,64]{1,0:T(8,128)}), f32[1440,64]{1,0:T(8,128)}) %reduce-scatter.13.cloned.1.call-update) | async-done | bytes 368656 | tf_op jit(solution)/shard_map/while
  1408.5 36.8 %reduce-scatter.13.cloned.1.call-done = f32[1440,64]{1,0:T(8,128)} async-done(((f32[5760,64]{1,0:T(8,128)}), f32[1440,64]{1,0:T(8,128)}) %reduce-scatter.13.cloned.1.call-update) | async-done | bytes 368656 | tf_op jit(solution)/shard_map/while
  1615.4 36.9 %reduce-scatter.13.cloned.1.call-done = f32[1440,64]{1,0:T(8,128)} async-done(((f32[5760,64]{1,0:T(8,128)}), f32[1440,64]{1,0:T(8,128)}) %reduce-scatter.13.cloned.1.call-update) | async-done | bytes 368656 | tf_op jit(solution)/shard_map/while
  1753.4 36.8 %reduce-scatter.13.cloned.1.call-done = f32[1440,64]{1,0:T(8,128)} async-done(((f32[5760,64]{1,0:T(8,128)}), f32[1440,64]{1,0:T(8,128)}) %reduce-scatter.13.cloned.1.call-update) | async-done | bytes 368656 | tf_op jit(solution)/shard_map/while
  1822.3 36.8 %reduce-scatter.13.cloned.1.call-done = f32[1440,64]{1,0:T(8,128)} async-done(((f32[5760,64]{1,0:T(8,128)}), f32[1440,64]{1,0:T(8,128)}) %reduce-scatter.13.cloned.1.call-update) | async-done | bytes 368656 | tf_op jit(solution)/shard_map/while
  1960.3 36.8 %reduce-scatter.13.cloned.1.call-done = f32[1440,64]{1,0:T(8,128)} async-done(((f32[5760,64]{1,0:T(8,128)}), f32[1440,64]{1,0:T(8,128)}) %reduce-scatter.13.cloned.1.call-update) | async-done | bytes 368656 | tf_op jit(solution)/shard_map/while
  2098.2 36.8 %reduce-scatter.13.cloned.1.call-done = f32[1440,64]{1,0:T(8,128)} async-done(((f32[5760,64]{1,0:T(8,128)}), f32[1440,64]{1,0:T(8,128)}) %reduce-scatter.13.cloned.1.call-update) | async-done | bytes 368656 | tf_op jit(solution)/shard_map/while
  (456 shorter events, 1398.2 us)
Async XLA Ops:
  9.7 55.1 %reduce-scatter.11.cloned.1.call-start = ((), (), s32[]{:S(2)}) async-start(), calls=%async_computation.2 | async-start | bytes 3686400 | tf_op jit(solution)/shard_map/while
  81.1 52.8 %reduce-scatter.11.cloned.1.call-start = ((), (), s32[]{:S(2)}) async-start(), calls=%async_computation.2 | async-start | bytes 3686400 | tf_op jit(solution)/shard_map/while
  219.1 52.8 %reduce-scatter.11.cloned.1.call-start = ((), (), s32[]{:S(2)}) async-start(), calls=%async_computation.2 | async-start | bytes 3686400 | tf_op jit(solution)/shard_map/while
  357.1 52.8 %reduce-scatter.11.cloned.1.call-start = ((), (), s32[]{:S(2)}) async-start(), calls=%async_computation.2 | async-start | bytes 3686400 | tf_op jit(solution)/shard_map/while
  426.1 52.8 %reduce-scatter.11.cloned.1.call-start = ((), (), s32[]{:S(2)}) async-start(), calls=%async_computation.2 | async-start | bytes 3686400 | tf_op jit(solution)/shard_map/while
  495.1 52.8 %reduce-scatter.11.cloned.1.call-start = ((), (), s32[]{:S(2)}) async-start(), calls=%async_computation.2 | async-start | bytes 3686400 | tf_op jit(solution)/shard_map/while
  564.1 52.8 %reduce-scatter.11.cloned.1.call-start = ((), (), s32[]{:S(2)}) async-start(), calls=%async_computation.2 | async-start | bytes 3686400 | tf_op jit(solution)/shard_map/while
  771.1 52.8 %reduce-scatter.11.cloned.1.call-start = ((), (), s32[]{:S(2)}) async-start(), calls=%async_computation.2 | async-start | bytes 3686400 | tf_op jit(solution)/shard_map/while
  909.0 52.8 %reduce-scatter.11.cloned.1.call-start = ((), (), s32[]{:S(2)}) async-start(), calls=%async_computation.2 | async-start | bytes 3686400 | tf_op jit(solution)/shard_map/while
  1047.1 52.8 %reduce-scatter.11.cloned.1.call-start = ((), (), s32[]{:S(2)}) async-start(), calls=%async_computation.2 | async-start | bytes 3686400 | tf_op jit(solution)/shard_map/while
  1185.6 52.8 %reduce-scatter.13.cloned.1.call-start = ((), (), s32[]{:S(2)}) async-start(), calls=%async_computation.3 | async-start | bytes 3686400 | tf_op jit(solution)/shard_map/while
  1254.6 52.8 %reduce-scatter.13.cloned.1.call-start = ((), (), s32[]{:S(2)}) async-start(), calls=%async_computation.3 | async-start | bytes 3686400 | tf_op jit(solution)/shard_map/while
  1392.6 52.8 %reduce-scatter.13.cloned.1.call-start = ((), (), s32[]{:S(2)}) async-start(), calls=%async_computation.3 | async-start | bytes 3686400 | tf_op jit(solution)/shard_map/while
  1461.5 52.8 %reduce-scatter.13.cloned.1.call-start = ((), (), s32[]{:S(2)}) async-start(), calls=%async_computation.3 | async-start | bytes 3686400 | tf_op jit(solution)/shard_map/while
  1530.5 52.8 %reduce-scatter.13.cloned.1.call-start = ((), (), s32[]{:S(2)}) async-start(), calls=%async_computation.3 | async-start | bytes 3686400 | tf_op jit(solution)/shard_map/while
  1599.4 52.8 %reduce-scatter.13.cloned.1.call-start = ((), (), s32[]{:S(2)}) async-start(), calls=%async_computation.3 | async-start | bytes 3686400 | tf_op jit(solution)/shard_map/while
  1668.4 52.8 %reduce-scatter.13.cloned.1.call-start = ((), (), s32[]{:S(2)}) async-start(), calls=%async_computation.3 | async-start | bytes 3686400 | tf_op jit(solution)/shard_map/while
  1737.4 52.8 %reduce-scatter.13.cloned.1.call-start = ((), (), s32[]{:S(2)}) async-start(), calls=%async_computation.3 | async-start | bytes 3686400 | tf_op jit(solution)/shard_map/while
  1806.4 52.8 %reduce-scatter.13.cloned.1.call-start = ((), (), s32[]{:S(2)}) async-start(), calls=%async_computation.3 | async-start | bytes 3686400 | tf_op jit(solution)/shard_map/while
  1875.4 52.8 %reduce-scatter.13.cloned.1.call-start = ((), (), s32[]{:S(2)}) async-start(), calls=%async_computation.3 | async-start | bytes 3686400 | tf_op jit(solution)/shard_map/while
  1944.4 52.8 %reduce-scatter.13.cloned.1.call-start = ((), (), s32[]{:S(2)}) async-start(), calls=%async_computation.3 | async-start | bytes 3686400 | tf_op jit(solution)/shard_map/while
  2013.3 52.8 %reduce-scatter.13.cloned.1.call-start = ((), (), s32[]{:S(2)}) async-start(), calls=%async_computation.3 | async-start | bytes 3686400 | tf_op jit(solution)/shard_map/while
  2082.3 52.8 %reduce-scatter.13.cloned.1.call-start = ((), (), s32[]{:S(2)}) async-start(), calls=%async_computation.3 | async-start | bytes 3686400 | tf_op jit(solution)/shard_map/while
  2151.3 52.8 %reduce-scatter.13.cloned.1.call-start = ((), (), s32[]{:S(2)}) async-start(), calls=%async_computation.3 | async-start | bytes 3686400 | tf_op jit(solution)/shard_map/while
  (44 other events, 1869.1 us)
Sparse Core Ops, SparseCore 0:
  25.8 39.0 reduce-scatter.10
  97.1 36.7 reduce-scatter.10
  166.1 36.6 reduce-scatter.10
  235.1 36.7 reduce-scatter.10
  304.1 36.6 reduce-scatter.10
  373.1 36.7 reduce-scatter.10
  442.1 36.7 reduce-scatter.10
  511.1 36.7 reduce-scatter.10
  580.1 36.7 reduce-scatter.10
  649.1 36.7 reduce-scatter.10
  718.1 36.7 reduce-scatter.10
  787.1 36.7 reduce-scatter.10
  856.1 36.6 reduce-scatter.10
  925.1 36.7 reduce-scatter.10
  994.1 36.6 reduce-scatter.10
  1063.1 36.7 reduce-scatter.10
  1132.7 36.6 reduce-scatter.12
  1201.7 36.7 reduce-scatter.12
  1408.6 36.6 reduce-scatter.12
  1615.5 36.7 reduce-scatter.12
  1753.5 36.6 reduce-scatter.12
  1822.5 36.6 reduce-scatter.12
  1960.4 36.6 reduce-scatter.12
  2098.4 36.6 reduce-scatter.12
  (8 shorter events, 293.0 us)
where the time goes:
time: 2230 us
  waiting for transfers between devices  1180 us (53%)
  blocking collectives  435 us (20%)
  matrix products  384 us (17%)
  local copies, waits for them, and re-layouts  191 us (9%)
    while x64, waiting for transfers between devices  1180 us
    all_gather x32, blocking collectives, lstm_step(): h_next = lax.all_gather(h_own, 'col', axis=1, tiled=True)  435 us
    dot_general x32, matrix products, lstm_step(): part_sum = jnp.dot(in_step, w_in, preferred_element_type=jnp.float32)  287 us
    while x160, local copies, waits for them, and re-layouts  172 us
    dot_general x32, matrix products, lstm_step(): jnp.dot(h_prev, w_rec, preferred_element_type=jnp.float32)  96.7 us
  transfers between devices with their start and end apart: 32, of which 32 were waited for; matrix products, arithmetic and copies ran while one was open for 0% of the time, Pallas kernels for 0%

commit v1 on v0

v1 whole, which is shorter than its diff:
```python
import jax
import jax.numpy as jnp
from jax import lax
from jax.experimental import pallas as pl
from jax.experimental.pallas import tpu as pltpu
from jax.sharding import PartitionSpec as P

MESH = pl.DeviceIdType.MESH
F32 = jnp.float32
BF16 = jnp.bfloat16
LANES = 128
ROW_CHUNK = 16


def lstm_kernel(steps, batch, n, rows_dev, cols_dev, width, pad_n,
                pin_hbm, w1_hbm, w2i_hbm, w2r_hbm, h0_ref, c0_ref, bias_ref,
                h2_out, c1_out, c2_out,
                w1, w2i, w2r, pin, hrow, cell, hblk, zb, rd, yr,
                w_sem, pin_sem, d_send, d_recv, y_send, y_recv, a_send, a_recv):
    row = lax.axis_index("row")
    col = lax.axis_index("col")
    core = lax.rem(row, 2)
    ypos = row // 2
    sibling = ypos * 2 + (1 - core)
    across = (1 - ypos) * 2 + core
    owners = ((1 - ypos) * 2 + (1 - core), across, sibling, row)
    tile_step = (n * 4) // LANES * LANES

    w_copies = [pltpu.make_async_copy(src, dst, w_sem.at[j])
                for j, (src, dst) in enumerate(((w1_hbm, w1), (w2i_hbm, w2i), (w2r_hbm, w2r)))]
    for cp in w_copies:
        cp.start()

    def pin_copy(step):
        slot = lax.rem(step, 2)
        return pltpu.make_async_copy(pin_hbm.at[step], pin.at[slot], pin_sem.at[slot])

    pin_copy(0).start()

    barrier = pltpu.get_barrier_semaphore()
    for peer_row in (sibling, across):
        pl.semaphore_signal(barrier, inc=1, device_id={"row": peer_row}, device_id_type=MESH)
    for j in (1, 2, 3):
        pl.semaphore_signal(barrier, inc=1, device_id={"col": lax.rem(col + j, 4)}, device_id_type=MESH)

    for layer in range(2):
        hrow[layer] = h0_ref[layer]
        cell[layer] = c0_ref[layer]
    pl.semaphore_wait(barrier, 5)

    def d2d(layer, par, half):
        return pltpu.make_async_remote_copy(
            src_ref=zb.at[layer, 2 * half], dst_ref=rd.at[layer, par, half],
            send_sem=d_send.at[layer, half], recv_sem=d_recv.at[layer, par, half],
            device_id={"row": sibling}, device_id_type=MESH)

    def ysum(layer, par):
        return pltpu.make_async_remote_copy(
            src_ref=zb.at[layer, 1], dst_ref=yr.at[layer, par],
            send_sem=y_send.at[layer], recv_sem=y_recv.at[layer, par],
            device_id={"row": across}, device_id_type=MESH)

    def gather(layer, par, j, src_col):
        return pltpu.make_async_remote_copy(
            src_ref=hblk.at[layer, par, src_col], dst_ref=hblk.at[layer, par, src_col],
            send_sem=a_send.at[layer, j], recv_sem=a_recv.at[layer, par, src_col],
            device_id={"col": lax.rem(col + j, 4)}, device_id_type=MESH)

    def gather_start(layer, par):
        for j in (1, 2, 3):
            gather(layer, par, j, col).start()

    def gather_wait_send(layer, par):
        for j in (1, 2, 3):
            gather(layer, par, j, col).wait_send()

    def assemble(layer, par):
        for j in (1, 2, 3):
            gather(layer, par, j, lax.rem(col + j, 4)).wait_recv()
        for q in range(0, batch, ROW_CHUNK):
            rows = pl.ds(q, ROW_CHUNK)
            tiles = [None] * (width // LANES)
            for k in range(4):
                first, off = (k * n) // LANES, (k * n) % LANES
                block = hblk[layer, par, k, rows, :].astype(F32)
                if off:
                    block = jnp.concatenate([block, jnp.zeros((ROW_CHUNK, LANES), F32)], axis=1)
                    block = pltpu.roll(block, off, axis=1)
                for t in range(block.shape[1] // LANES):
                    piece = block[:, t * LANES:(t + 1) * LANES]
                    held = tiles[first + t]
                    tiles[first + t] = piece if held is None else held + piece
            for t, piece in enumerate(tiles):
                hrow[layer, rows, t * LANES:(t + 1) * LANES] = piece.astype(BF16)

    def columns(i):
        return pl.ds(pl.multiple_of(owners[i] * tile_step, LANES), width)

    def dot_block(layer, weights, i):
        return jnp.dot(hrow[layer, :, :rows_dev], weights[:, columns(i)], preferred_element_type=F32)

    def reduce_first(layer, par):
        d2d(layer, par, 0).wait_recv()
        zb[layer, 1] = zb[layer, 1] + rd[layer, par, 0]
        ysum(layer, par).start()

    def cell_update(layer, par):
        d2d(layer, par, 1).wait_recv()
        ysum(layer, par).wait_recv()
        span = pad_n + LANES
        lane = lax.broadcasted_iota(jnp.int32, (ROW_CHUNK, pad_n), 1)
        start0 = row * (4 * n - tile_step)
        for q in range(0, batch, ROW_CHUNK):
            rows = pl.ds(q, ROW_CHUNK)
            gates = []
            for m in range(4):
                start = start0 + m * n
                tile = jnp.minimum(start // LANES, (width - span) // LANES)
                shift = start - tile * LANES
                at = pl.ds(pl.multiple_of(tile * LANES, LANES), span)
                z = zb[layer, 3, rows, at] + rd[layer, par, 1, rows, at] + yr[layer, par, rows, at]
                z = pltpu.roll(z, span - shift, axis=1)[:, :pad_n]
                gates.append(z + bias_ref[layer, m:m + 1, :])
            c_new = (jax.nn.sigmoid(gates[1]) * cell[layer, rows, :]
                     + jax.nn.sigmoid(gates[0]) * jnp.tanh(gates[2]))
            cell[layer, rows, :] = c_new
            h_new = jax.nn.sigmoid(gates[3]) * jnp.tanh(c_new)
            hblk[layer, par, col, rows, :] = jnp.where(lane < n, h_new, 0.0).astype(BF16)

    def wait_sum_sends(layer, par):
        d2d(layer, par, 0).wait_send()
        d2d(layer, par, 1).wait_send()
        ysum(layer, par).wait_send()

    def step_body(s, carry):
        par = lax.rem(s, 2)
        prev = 1 - par

        @pl.when(s > 0)
        def _():
            assemble(0, prev)

        @pl.when(s < steps)
        def _():
            pin_copy(s).wait()

            @pl.when(s + 1 < steps)
            def _():
                pin_copy(s + 1).start()

            @pl.when(s == 0)
            def _():
                w_copies[0].wait()

            for i in range(4):
                zb[0, i] = dot_block(0, w1, i) + pin[par, :, columns(i)]
                if i % 2 == 0:
                    d2d(0, par, i // 2).start()
                if i == 2:
                    reduce_first(0, par)

        @pl.when(s == 1)
        def _():
            w_copies[1].wait()
            w_copies[2].wait()

        @pl.when(s >= 2)
        def _():
            @pl.when(s >= 3)
            def _():
                gather_wait_send(1, prev)

            cell_update(1, par)
            h2_out[s - 2] = hblk[1, par, col, :, :n]
            gather_start(1, par)
            wait_sum_sends(1, par)

        @pl.when(s >= 1)
        def _():
            for i in range(4):
                zb[1, i] = dot_block(0, w2i, i)

            @pl.when(s >= 2)
            def _():
                assemble(1, par)

            for i in range(4):
                zb[1, i] = zb[1, i] + dot_block(1, w2r, i)
                if i % 2 == 0:
                    d2d(1, prev, i // 2).start()
                if i == 2:
                    reduce_first(1, prev)

        @pl.when(s < steps)
        def _():
            @pl.when(s >= 1)
            def _():
                gather_wait_send(0, prev)

            cell_update(0, par)
            gather_start(0, par)
            wait_sum_sends(0, par)

        return carry

    lax.fori_loop(0, steps + 1, step_body, 0)

    last = (steps - 1) % 2
    gather_wait_send(1, 1 - last)
    gather_wait_send(0, last)
    cell_update(1, last)
    h2_out[steps - 1] = hblk[1, last, col, :, :n]
    wait_sum_sends(1, last)
    c1_out[...] = cell[0, :, :n]
    c2_out[...] = cell[1, :, :n]


def solution(mesh):
    def local_program(seq_in, w_in1, w_rec1, b_gate1, w_in2, w_rec2, b_gate2, h_init, c_init):
        steps, batch, rows_dev = seq_in.shape
        cols_dev = w_in1.shape[1]
        n = b_gate1.shape[0] // 4
        pad_n = -(-n // LANES) * LANES
        width = -(-rows_dev // LANES) * LANES

        pin = jnp.dot(seq_in.reshape(steps * batch, rows_dev), w_in1, preferred_element_type=F32)
        pin = pin.reshape(steps, batch, cols_dev)
        h0 = jnp.pad(h_init.astype(BF16), ((0, 0), (0, 0), (0, width - rows_dev)))
        c0 = lax.dynamic_slice_in_dim(c_init, lax.axis_index("col") * n, n, axis=2)
        c0 = jnp.pad(c0, ((0, 0), (0, 0), (0, pad_n - n)))
        bias = jnp.stack([b_gate1, b_gate2]).reshape(2, 4, n)
        bias = jnp.pad(bias, ((0, 0), (0, 0), (0, pad_n - n)))

        def kernel(*refs):
            lstm_kernel(steps, batch, n, rows_dev, cols_dev, width, pad_n, *refs)

        hbm = pl.BlockSpec(memory_space=pl.ANY)
        vmem = pl.BlockSpec(memory_space=pltpu.VMEM)
        dma = pltpu.SemaphoreType.DMA
        return pl.pallas_call(
            kernel,
            name="lstm_grid",
            out_shape=(jax.ShapeDtypeStruct((steps, batch, n), BF16),
                       jax.ShapeDtypeStruct((batch, n), F32),
                       jax.ShapeDtypeStruct((batch, n), F32)),
            in_specs=[hbm] * 4 + [vmem] * 3,
            out_specs=(vmem, vmem, vmem),
            scratch_shapes=[
                pltpu.VMEM((rows_dev, cols_dev), BF16),
                pltpu.VMEM((rows_dev, cols_dev), BF16),
                pltpu.VMEM((rows_dev, cols_dev), BF16),
                pltpu.VMEM((2, batch, cols_dev), F32),
                pltpu.VMEM((2, batch, width), BF16),
                pltpu.VMEM((2, batch, pad_n), F32),
                pltpu.VMEM((2, 2, 4, batch, pad_n), BF16),
                pltpu.VMEM((2, 4, batch, width), F32),
                pltpu.VMEM((2, 2, 2, batch, width), F32),
                pltpu.VMEM((2, 2, batch, width), F32),
                dma((3,)), dma((2,)),
                dma((2, 2)), dma((2, 2, 2)),
                dma((2,)), dma((2, 2)),
                dma((2, 3 + 1)), dma((2, 2, 4)),
            ],
            compiler_params=pltpu.CompilerParams(
                collective_id=0, has_side_effects=True, vmem_limit_bytes=67043328),
        )(pin, w_rec1, w_in2, w_rec2, h0, c0, bias)

    row_spec = P(None, "dp", "row")
    weight_spec = P("row", "col")
    bias_spec = P(("col", "row"))
    seq_out_spec = P(None, "dp", ("row", "col"))
    cell_out_spec = P("dp", ("row", "col"))
    return jax.shard_map(
        local_program,
        mesh=mesh,
        in_specs=(row_spec, weight_spec, weight_spec, bias_spec, weight_spec, weight_spec, bias_spec, row_spec, row_spec),
        out_specs=(seq_out_spec, cell_out_spec, cell_out_spec),
        check_vma=False,
    )
```

time: 2230 us -> 395 us (0.18)
  waiting for transfers between devices: 1180 us -> 0 us
  blocking collectives: 435 us -> 0 us
  matrix products: 384 us -> 25.7 us
  Pallas kernels: 0 us -> 357 us
  local copies, waits for them, and re-layouts: 191 us -> 9.24 us
    while x64 -> x0, waiting for transfers between devices: 1180 us -> none
    all_gather x32 -> x0, blocking collectives: 435 us -> none  [lstm_step(): h_next = lax.all_gather(h_own, 'col', axis=1, tiled=True)]
    dot_general x64 -> x1, matrix products: 384 us -> 25.7 us  [local_program(): jnp.dot(seq_in.reshape(steps * batch, rows_dev), w_in1, preferred_element...]
    pallas_call x0 -> x1, Pallas kernels: none -> 357 us  [local_program(): pl.pallas_call(kernel, name='lstm_grid', out_shape=(jax.ShapeDtypeStruct(...]
    while x160 -> x0, local copies, waits for them, and re-layouts: 172 us -> none
  transfers between devices with their start and end apart: 32 -> 0, of which waited for: 32 -> 0; matrix products, arithmetic and copies ran while one was open for 0% -> 0% of each run, Pallas kernels for 0% -> 0%
where the time goes in v1:
time: 395 us
  Pallas kernels  357 us (90%)
  matrix products  25.7 us (7%)
  local copies, waits for them, and re-layouts  9.24 us (2%)
    pallas_call x1, Pallas kernels, local_program(): pl.pallas_call(kernel, name='lstm_grid', out_shape=(jax.ShapeDtypeStruct(...  357 us
    dot_general x1, matrix products, local_program(): jnp.dot(seq_in.reshape(steps * batch, rows_dev), w_in1, preferred_element...  25.7 us

profile of v1, /device:TPU:0, one launch (start us, length us, event | category | flops | bytes accessed | tf_op | source)
XLA Modules:
  0.0 394.8 jit_solution(4278609520641401676)
XLA Ops:
  0.6 0.8 stack.9
  1.4 0.8 stack.10
  2.2 0.6 select_maximum_fusion.refs_6_
  2.8 1.1 constant_dynamic-slice_fusion
  3.9 0.7 pad.13.refs_5_
  4.5 1.2 convert_element_type.9
  5.7 0.8 pad.12.refs_4_
  6.5 25.7 %fusion.refs_0_ = f32[16,64,5760]{2,1,0:T(8,128)} fusion(bf16[16,64,1440]{2,1,0:T(8,128)(2,1)} %param.9, bf16[1440,5760]{1,0:T(8,128)(2,1)} %param.10), kind=kOutput, calls=%fused_computation | convolution fusion | flops 16986931200 | bytes 43130880 | tf_op jit(solution)/shard_map/dot_general | solution.py:226
  32.2 357.4 %lstm_grid.1 = (bf16[16,64,360]{2,1,0:T(8,128)(2,1)}, f32[64,360]{1,0:T(8,128)}, f32[64,360]{1,0:T(8,128)}) custom-call(f32[16,64,5760]{2,1,0:T(8,128)} %fusion.refs_0_, bf16[1440,5760]{1,0:T(8,128)(2,1)} %refs_1_.1, bf16[1440,5760]{1,0:T(8,128)(2,1)} %refs_2_.1, bf16[1440,5760]{1,0:T(8,128)(2,1)} %refs_3_.1, bf16[2,64,1536]{2,1,0:T(8,128)(2,1)} %pad.12.refs_4_, ...), custom_call_target="tpu_custom_call" | custom-call | tf_op jit(solution)/shard_map/lstm_grid/pallas_call | solution.py:240
  389.7 2.1 copy.15
  391.8 1.5 copy.16
  393.3 1.5 copy.17

commit v2 on v1

v2 whole, which is shorter than its diff:
```python
import jax
import jax.numpy as jnp
from jax import lax
from jax.experimental import pallas as pl
from jax.experimental.pallas import tpu as pltpu
from jax.sharding import PartitionSpec as P

MESH = pl.DeviceIdType.MESH
F32 = jnp.float32
BF16 = jnp.bfloat16
LANES = 128
ROW_CHUNK = 8
PIECES = ((0, 32), (32, 24), (56, 8))
STRIP = 512


def lstm_kernel(steps, batch, n, rows_dev, cols_dev, width, pad_n,
                pin_hbm, w1_hbm, w2i_hbm, w2r_hbm, h0_ref, c0_ref, bias_ref,
                h2_out, c1_out, c2_out,
                w1, w2i, w2r, pin, cell, hblk, zb, rd, yr,
                w_sem, pin_sem, d_send, d_recv, y_send, y_recv, a_send, a_recv):
    row = lax.axis_index("row")
    col = lax.axis_index("col")
    core = lax.rem(row, 2)
    ypos = row // 2
    sibling = ypos * 2 + (1 - core)
    across = (1 - ypos) * 2 + core
    owners = ((1 - ypos) * 2 + (1 - core), across, sibling, row)
    tile_step = (n * 4) // LANES * LANES
    strips = tuple(range(0, width, STRIP))

    w_copies = [pltpu.make_async_copy(src, dst, w_sem.at[j])
                for j, (src, dst) in enumerate(((w1_hbm, w1), (w2i_hbm, w2i), (w2r_hbm, w2r)))]
    for cp in w_copies:
        cp.start()

    def pin_copy(step):
        slot = lax.rem(step, 2)
        return pltpu.make_async_copy(pin_hbm.at[step], pin.at[slot], pin_sem.at[slot])

    pin_copy(0).start()

    barrier = pltpu.get_barrier_semaphore()
    for peer_row in (sibling, across):
        pl.semaphore_signal(barrier, inc=1, device_id={"row": peer_row}, device_id_type=MESH)
    for j in (1, 2, 3):
        pl.semaphore_signal(barrier, inc=1, device_id={"col": lax.rem(col + j, 4)}, device_id_type=MESH)

    for layer in range(2):
        hblk[layer, 1] = h0_ref[layer]
        cell[layer] = c0_ref[layer]
    pl.semaphore_wait(barrier, 5)

    def d2d(layer, par, j):
        if j < len(strips):
            src, dst = zb.at[layer, 0, :, pl.ds(strips[j], STRIP)], rd.at[layer, par, 0, :, pl.ds(strips[j], STRIP)]
        else:
            src, dst = zb.at[layer, 2], rd.at[layer, par, 1]
        return pltpu.make_async_remote_copy(
            src_ref=src, dst_ref=dst, send_sem=d_send.at[layer, j], recv_sem=d_recv.at[layer, par, j],
            device_id={"row": sibling}, device_id_type=MESH)

    def ysum(layer, par, j):
        if j < len(strips):
            at = (pl.ds(*PIECES[0]), pl.ds(strips[j], STRIP))
        else:
            at = (pl.ds(*PIECES[j - len(strips) + 1]), slice(None))
        return pltpu.make_async_remote_copy(
            src_ref=zb.at[(layer, 1) + at], dst_ref=yr.at[(layer, par) + at],
            send_sem=y_send.at[layer, j], recv_sem=y_recv.at[layer, par, j],
            device_id={"row": across}, device_id_type=MESH)

    y_copies = len(strips) + len(PIECES) - 1

    far = 3 * (1 - col // 2)
    near = 1 + lax.rem(col, 2)
    others = (far, 6 - col - far - near, near)

    def gather(layer, piece, par, j, src_col):
        at = (layer, par, src_col, pl.ds(*PIECES[piece]))
        return pltpu.make_async_remote_copy(
            src_ref=hblk.at[at], dst_ref=hblk.at[at],
            send_sem=a_send.at[layer, piece, j], recv_sem=a_recv.at[layer, par, piece, src_col],
            device_id={"col": others[j]}, device_id_type=MESH)

    def gather_start(layer, piece, par):
        for j in range(3):
            gather(layer, piece, par, j, col).start()

    def gather_wait_send(layer, par):
        for piece in range(len(PIECES)):
            for j in range(3):
                gather(layer, piece, par, j, col).wait_send()

    def gather_wait(layer, par):
        for piece in range(len(PIECES)):
            for j in range(3):
                gather(layer, piece, par, j, others[j]).wait_recv()

    def columns(i, start, size):
        return pl.ds(pl.multiple_of(owners[i] * tile_step + start, LANES), size)

    def dot_block(layer, par, weights, i, start, size):
        total = None
        for k in range(4):
            part = jnp.dot(hblk[layer, par, k, :, :n], weights[k * n:(k + 1) * n, columns(i, start, size)],
                           preferred_element_type=F32)
            total = part if total is None else total + part
        return total

    def send_sums(layer, par, block, between):
        def strip(i, j):
            zb[layer, i, :, strips[j]:strips[j] + STRIP] = block(i, strips[j], STRIP)

        for j in range(len(strips)):
            strip(0, j)
            d2d(layer, par, j).start()
        for j in range(len(strips)):
            strip(1, j)
            d2d(layer, par, j).wait_recv()
            at = slice(strips[j], strips[j] + STRIP)
            zb[layer, 1, :, at] = zb[layer, 1, :, at] + rd[layer, par, 0, :, at]
            ysum(layer, par, j).start()
        for j in range(len(strips), y_copies):
            ysum(layer, par, j).start()
        zb[layer, 2] = block(2, 0, width)
        d2d(layer, par, len(strips)).start()
        between()
        zb[layer, 3] = block(3, 0, width)

    def cell_update(layer, piece, par, step):
        if piece == 0:
            d2d(layer, par, len(strips)).wait_recv()
            for j in range(len(strips)):
                ysum(layer, par, j).wait_recv()
        else:
            ysum(layer, par, len(strips) + piece - 1).wait_recv()
        span = pad_n + LANES
        lane = lax.broadcasted_iota(jnp.int32, (ROW_CHUNK, pad_n), 1)
        start0 = row * (4 * n - tile_step)
        first, size = PIECES[piece]
        for q in range(first, first + size, ROW_CHUNK):
            rows = pl.ds(q, ROW_CHUNK)
            gates = []
            for m in range(4):
                start = start0 + m * n
                tile = jnp.minimum(start // LANES, (width - span) // LANES)
                shift = start - tile * LANES
                at = pl.ds(pl.multiple_of(tile * LANES, LANES), span)
                z = zb[layer, 3, rows, at] + rd[layer, par, 1, rows, at] + yr[layer, par, rows, at]
                z = pltpu.roll(z, span - shift, axis=1)[:, :pad_n]
                gates.append(z + bias_ref[layer, m:m + 1, :])
            c_new = (jax.nn.sigmoid(gates[1]) * cell[layer, rows, :]
                     + jax.nn.sigmoid(gates[0]) * jnp.tanh(gates[2]))
            cell[layer, rows, :] = c_new
            h_new = jnp.where(lane < n, jax.nn.sigmoid(gates[3]) * jnp.tanh(c_new), 0.0).astype(BF16)
            hblk[layer, par, col, rows, :] = h_new
            if layer == 1:
                h2_out[step, rows, :] = h_new[:, :n]

    def wait_sum_sends(layer, par):
        for j in range(len(strips) + 1):
            d2d(layer, par, j).wait_send()
        for j in range(y_copies):
            ysum(layer, par, j).wait_send()

    def finish(layer, piece, par, step, first):
        if piece == 0:
            @pl.when(jnp.logical_not(first))
            def _():
                gather_wait_send(layer, 1 - par)

        cell_update(layer, piece, par, step)
        gather_start(layer, piece, par)
        if piece == len(PIECES) - 1:
            wait_sum_sends(layer, par)

    def step_body(s, carry):
        par = lax.rem(s, 2)
        prev = 1 - par

        def finish_two():
            @pl.when(s >= 2)
            def _():
                finish(1, 1, par, s - 2, s == 2)

        @pl.when(s > 0)
        def _():
            gather_wait(0, prev)

        @pl.when(s < steps)
        def _():
            pin_copy(s).wait()

            @pl.when(s + 1 < steps)
            def _():
                pin_copy(s + 1).start()

            @pl.when(s == 0)
            def _():
                w_copies[0].wait()

            send_sums(0, par, lambda i, start, size: dot_block(0, prev, w1, i, start, size)
                      + pin[par, :, columns(i, start, size)], finish_two)

        @pl.when(s == steps)
        def _():
            finish_two()

        @pl.when(s >= 2)
        def _():
            finish(1, 2, par, s - 2, s == 2)

        @pl.when(s == 1)
        def _():
            w_copies[1].wait()
            w_copies[2].wait()

        @pl.when(s >= 1)
        def _():
            for i in range(4):
                zb[1, i] = dot_block(0, prev, w2i, i, 0, width)

        @pl.when(s < steps)
        def _():
            finish(0, 0, par, s, s == 0)

        def finish_one():
            @pl.when(s < steps)
            def _():
                finish(0, 1, par, s, s == 0)

        @pl.when(s >= 1)
        def _():
            @pl.when(s >= 2)
            def _():
                gather_wait(1, par)

            send_sums(1, prev, lambda i, start, size: zb[1, i, :, start:start + size]
                      + dot_block(1, par, w2r, i, start, size), finish_one)

        @pl.when(s == 0)
        def _():
            finish_one()

        @pl.when(s < steps)
        def _():
            finish(0, 2, par, s, s == 0)

        @pl.when(jnp.logical_and(s >= 1, s < steps))
        def _():
            finish(1, 0, prev, s - 1, s == 1)

        return carry

    lax.fori_loop(0, steps + 1, step_body, 0)

    last = (steps - 1) % 2
    gather_wait_send(1, 1 - last)
    gather_wait_send(0, last)
    for piece in range(len(PIECES)):
        cell_update(1, piece, last, steps - 1)
    wait_sum_sends(1, last)
    c1_out[...] = cell[0, :, :n]
    c2_out[...] = cell[1, :, :n]


def solution(mesh):
    def local_program(seq_in, w_in1, w_rec1, b_gate1, w_in2, w_rec2, b_gate2, h_init, c_init):
        steps, batch, rows_dev = seq_in.shape
        cols_dev = w_in1.shape[1]
        n = b_gate1.shape[0] // 4
        pad_n = -(-n // LANES) * LANES
        width = -(-rows_dev // LANES) * LANES

        pin = jnp.dot(seq_in.reshape(steps * batch, rows_dev), w_in1, preferred_element_type=F32)
        pin = pin.reshape(steps, batch, cols_dev)
        h0 = h_init.astype(BF16).reshape(2, batch, 4, n).transpose(0, 2, 1, 3)
        h0 = jnp.pad(h0, ((0, 0), (0, 0), (0, 0), (0, pad_n - n)))
        c0 = lax.dynamic_slice_in_dim(c_init, lax.axis_index("col") * n, n, axis=2)
        c0 = jnp.pad(c0, ((0, 0), (0, 0), (0, pad_n - n)))
        bias = jnp.stack([b_gate1, b_gate2]).reshape(2, 4, n)
        bias = jnp.pad(bias, ((0, 0), (0, 0), (0, pad_n - n)))

        def kernel(*refs):
            lstm_kernel(steps, batch, n, rows_dev, cols_dev, width, pad_n, *refs)

        hbm = pl.BlockSpec(memory_space=pl.ANY)
        vmem = pl.BlockSpec(memory_space=pltpu.VMEM)
        dma = pltpu.SemaphoreType.DMA
        strips, pieces = width // STRIP, len(PIECES)
        return pl.pallas_call(
            kernel,
            name="lstm_grid",
            out_shape=(jax.ShapeDtypeStruct((steps, batch, n), BF16),
                       jax.ShapeDtypeStruct((batch, n), F32),
                       jax.ShapeDtypeStruct((batch, n), F32)),
            in_specs=[hbm] * 4 + [vmem] * 3,
            out_specs=(vmem, vmem, vmem),
            scratch_shapes=[
                pltpu.VMEM((rows_dev, cols_dev), BF16),
                pltpu.VMEM((rows_dev, cols_dev), BF16),
                pltpu.VMEM((rows_dev, cols_dev), BF16),
                pltpu.VMEM((2, batch, cols_dev), F32),
                pltpu.VMEM((2, batch, pad_n), F32),
                pltpu.VMEM((2, 2, 4, batch, pad_n), BF16),
                pltpu.VMEM((2, 4, batch, width), F32),
                pltpu.VMEM((2, 2, 2, batch, width), F32),
                pltpu.VMEM((2, 2, batch, width), F32),
                dma((3,)), dma((2,)),
                dma((2, strips + 1)), dma((2, 2, strips + 1)),
                dma((2, strips + pieces - 1)), dma((2, 2, strips + pieces - 1)),
                dma((2, pieces, 3)), dma((2, 2, pieces, 4)),
            ],
            compiler_params=pltpu.CompilerParams(
                collective_id=0, has_side_effects=True, vmem_limit_bytes=67043328),
        )(pin, w_rec1, w_in2, w_rec2, h0, c0, bias)

    row_spec = P(None, "dp", "row")
    weight_spec = P("row", "col")
    bias_spec = P(("col", "row"))
    seq_out_spec = P(None, "dp", ("row", "col"))
    cell_out_spec = P("dp", ("row", "col"))
    return jax.shard_map(
        local_program,
        mesh=mesh,
        in_specs=(row_spec, weight_spec, weight_spec, bias_spec, weight_spec, weight_spec, bias_spec, row_spec, row_spec),
        out_specs=(seq_out_spec, cell_out_spec, cell_out_spec),
        check_vma=False,
    )
```

time: 395 us -> 352 us (0.89)
  Pallas kernels: 357 us -> 314 us
    pallas_call x1, Pallas kernels: 357 us -> 314 us  [local_program(): pl.pallas_call(kernel, name='lstm_grid', out_shape=(jax.ShapeDtypeStruct(...]
where the time goes in v2:
time: 352 us
  Pallas kernels  314 us (89%)
  matrix products  25.7 us (7%)
  local copies, waits for them, and re-layouts  9.72 us (3%)
    pallas_call x1, Pallas kernels, local_program(): pl.pallas_call(kernel, name='lstm_grid', out_shape=(jax.ShapeDtypeStruct(...  314 us
    dot_general x1, matrix products, local_program(): jnp.dot(seq_in.reshape(steps * batch, rows_dev), w_in1, preferred_element...  25.7 us

profile of v2, /device:TPU:0, one launch (start us, length us, event | category | flops | bytes accessed | tf_op | source)
XLA Modules:
  0.0 351.8 jit_solution(1268936213078680203)
XLA Ops:
  0.6 0.8 stack.9
  1.4 0.8 stack.10
  2.2 0.6 select_maximum_fusion.refs_6_
  2.8 1.1 constant_dynamic-slice_fusion
  3.9 0.7 pad.13.refs_5_
  4.5 1.2 convert_element_type.9
  5.7 0.4 reshape.18
  6.2 0.8 pad.12.refs_4_
  7.0 25.7 %fusion.refs_0_ = f32[16,64,5760]{2,1,0:T(8,128)} fusion(bf16[16,64,1440]{2,1,0:T(8,128)(2,1)} %param.9, bf16[1440,5760]{1,0:T(8,128)(2,1)} %param.10), kind=kOutput, calls=%fused_computation | convolution fusion | flops 16986931200 | bytes 43130880 | tf_op jit(solution)/shard_map/dot_general | solution.py:276
  32.7 313.9 %lstm_grid.1 = (bf16[16,64,360]{2,1,0:T(8,128)(2,1)}, f32[64,360]{1,0:T(8,128)}, f32[64,360]{1,0:T(8,128)}) custom-call(f32[16,64,5760]{2,1,0:T(8,128)} %fusion.refs_0_, bf16[1440,5760]{1,0:T(8,128)(2,1)} %refs_1_.1, bf16[1440,5760]{1,0:T(8,128)(2,1)} %refs_2_.1, bf16[1440,5760]{1,0:T(8,128)(2,1)} %refs_3_.1, bf16[2,4,64,384]{3,2,1,0:T(8,128)(2,1)} %pad.12.refs_4_, ...), custom_call_target="tpu_custom_call" | custom-call | tf_op jit(solution)/shard_map/lstm_grid/pallas_call | solution.py:292
  346.6 2.1 copy.18
  348.7 1.5 copy.19
  350.2 1.5 copy.20
  (1 shorter events, 0.0 us)

commit v3 on v2

v3 whole, which is shorter than its diff:
```python
import jax
import jax.numpy as jnp
from jax import lax
from jax.experimental import pallas as pl
from jax.experimental.pallas import tpu as pltpu
from jax.sharding import PartitionSpec as P

MESH = pl.DeviceIdType.MESH
F32 = jnp.float32
BF16 = jnp.bfloat16
LANES = 128
ROW_CHUNK = 8
PIECES = ((0, 32), (32, 24), (56, 8))
STRIPS = (((128, 512),), ((640, 512),), ((1152, 384), (0, 128)))
D2D_LANES = tuple(part for strip in STRIPS for part in strip)
GROUP = 4


def lstm_kernel(steps, batch, n, rows_dev, cols_dev, width, pad_n,
                seq_hbm, w1i_hbm, w1_hbm, w2i_hbm, w2r_hbm, h0_ref, c0_ref, b1_ref, b2_ref,
                h2_out, c1_out, c2_out, pin_hbm,
                w1, w2i, w2r, xbuf, pin, cell, bias, hblk, zb, rd, yr, es, er,
                w_sem, wi_sem, x_sem, st_sem, pin_sem, d_send, d_recv, y_send, y_recv, e_send, e_recv, a_send, a_recv):
    row = lax.axis_index("row")
    col = lax.axis_index("col")
    core = lax.rem(row, 2)
    ypos = row // 2
    sibling = ypos * 2 + (1 - core)
    across = (1 - ypos) * 2 + core
    owners = ((1 - ypos) * 2 + (1 - core), across, sibling, row)
    tile_step = (n * 4) // LANES * LANES
    edge = width - LANES
    lane = lax.broadcasted_iota(jnp.int32, (ROW_CHUNK, LANES), 1)

    w_copies = [pltpu.make_async_copy(src, dst, w_sem.at[j])
                for j, (src, dst) in enumerate(((w1_hbm, w1), (w2i_hbm, w2i), (w2r_hbm, w2r)))]

    spans = 4

    def span_at(j):
        return pl.ds(pl.multiple_of(jnp.minimum(j * width, cols_dev - width), LANES), width)

    def w1i_copy(j):
        at = pl.ds(j * width, min(width, cols_dev - j * width))
        return pltpu.make_async_copy(w1i_hbm.at[:, at], w2r.at[:, at], wi_sem.at[j])

    def x_copy(g):
        return pltpu.make_async_copy(seq_hbm.at[pl.ds(g * GROUP, GROUP)], xbuf.at[g % 2], x_sem.at[g % 2])

    def stage_copy(g, j, slot):
        src = zb.at[1] if slot == 0 else rd.at[1].reshape(GROUP, batch, width)
        return pltpu.make_async_copy(src, pin_hbm.at[pl.ds(g * GROUP, GROUP), :, span_at(j)], st_sem.at[slot])

    def project(g):
        x_copy(g).wait()
        if (g + 1) * GROUP < steps:
            x_copy(g + 1).start()

        def pair(jj, carry):
            for slot in range(2):
                j = 2 * jj + slot

                @pl.when(jj > 0)
                def _():
                    stage_copy(g, j - 2, slot).wait()

                z = jnp.dot(xbuf[g % 2].reshape(GROUP * batch, rows_dev), w2r[:, span_at(j)], preferred_element_type=F32)
                if slot == 0:
                    zb[1] = z.reshape(GROUP, batch, width)
                else:
                    rd[1] = z.reshape(2, 2, batch, width)
                    @pl.when(jj > 0)
                    def _():
                        stage_copy(g, j - 1, 0).wait()
                stage_copy(g, j, slot).start()
            return carry

        return pair

    def run_project(g):
        lax.fori_loop(0, spans // 2, project(g), 0)
        stage_copy(g, spans - 1, 1).wait()

    x_copy(0).start()
    for j in range(spans):
        w1i_copy(j).start()

    def pin_copy(step):
        slot = lax.rem(step, 2)
        return pltpu.make_async_copy(pin_hbm.at[step], pin.at[slot], pin_sem.at[slot])

    barrier = pltpu.get_barrier_semaphore()
    for peer_row in (sibling, across):
        pl.semaphore_signal(barrier, inc=1, device_id={"row": peer_row}, device_id_type=MESH)
    for j in (1, 2, 3):
        pl.semaphore_signal(barrier, inc=1, device_id={"col": lax.rem(col + j, 4)}, device_id_type=MESH)

    for layer in range(2):
        hblk[layer, 1, :, :, :n] = h0_ref[layer]
        cell[layer] = jnp.zeros((batch, pad_n), F32)
        cell[layer, :, :n] = c0_ref[layer]
        bias[layer] = jnp.zeros((8, pad_n), F32)
        bias[layer, :4, :n] = (b1_ref, b2_ref)[layer][...]
    first_pair = project(0)
    for jj in range(spans // 2):
        w1i_copy(2 * jj).wait()
        w1i_copy(2 * jj + 1).wait()
        first_pair(jj, 0)
        w_copies[jj].start()
    stage_copy(0, spans - 1, 1).wait()
    pin_copy(0).start()
    pl.semaphore_wait(barrier, 5)

    def d2d(layer, par, j):
        if j < len(D2D_LANES):
            at = pl.ds(*D2D_LANES[j])
            src, dst = zb.at[layer, 0, :, at], rd.at[layer, par, 0, :, at]
        else:
            src, dst = zb.at[layer, 2], rd.at[layer, par, 1]
        return pltpu.make_async_remote_copy(
            src_ref=src, dst_ref=dst, send_sem=d_send.at[layer, j], recv_sem=d_recv.at[layer, par, j],
            device_id={"row": sibling}, device_id_type=MESH)

    def ysum(layer, par, j):
        if j < len(STRIPS):
            at = (pl.ds(*PIECES[0]), pl.ds(*STRIPS[j][0]))
        else:
            at = (pl.ds(*PIECES[j - len(STRIPS) + 1]), pl.ds(LANES, edge))
        return pltpu.make_async_remote_copy(
            src_ref=zb.at[(layer, 1) + at], dst_ref=yr.at[(layer, par) + at],
            send_sem=y_send.at[layer, j], recv_sem=y_recv.at[layer, par, j],
            device_id={"row": across}, device_id_type=MESH)

    def yedge(layer, par, piece):
        return pltpu.make_async_remote_copy(
            src_ref=es.at[layer, piece], dst_ref=er.at[layer, par, piece],
            send_sem=e_send.at[layer, piece], recv_sem=e_recv.at[layer, par, piece],
            device_id={"row": across}, device_id_type=MESH)

    y_copies = len(STRIPS) + len(PIECES) - 1

    def pack_edges(layer, par):
        own = across * 32
        quarter = jnp.bitwise_and(jnp.right_shift(lane, 5) + 4 - across, 3)
        for piece, (first, size) in enumerate(PIECES):
            packed = None
            for g in range(size // ROW_CHUNK):
                rows = pl.ds(first + g * ROW_CHUNK, ROW_CHUNK)
                head = zb[layer, 1, rows, :LANES] + rd[layer, par, 0, rows, :LANES]
                tail = zb[layer, 1, rows, edge:] + rd[layer, par, 0, rows, edge:]
                zb[layer, 1, rows, edge:] = jnp.where(lane >= own, head, tail)
                moved = pltpu.roll(tail, 32 * g, axis=1) if g else tail
                packed = moved if packed is None else jnp.where(quarter == g, moved, packed)
            es[layer, piece] = packed

    def unpack_edges(layer, piece, par):
        own = row * 32
        packed = er[layer, par, piece]
        first, size = PIECES[piece]
        for g in range(size // ROW_CHUNK):
            rows = pl.ds(first + g * ROW_CHUNK, ROW_CHUNK)
            both = yr[layer, par, rows, edge:]
            moved = pltpu.roll(packed, LANES - 32 * g, axis=1) if g else packed
            yr[layer, par, rows, :LANES] = both
            yr[layer, par, rows, edge:] = jnp.where(lane < own, both, moved)

    far = 3 * (1 - col // 2)
    near = 1 + lax.rem(col, 2)
    others = (far, 6 - col - far - near, near)

    def gather(layer, piece, par, j, src_col):
        at = (layer, par, src_col, pl.ds(*PIECES[piece]))
        return pltpu.make_async_remote_copy(
            src_ref=hblk.at[at], dst_ref=hblk.at[at],
            send_sem=a_send.at[layer, piece, j], recv_sem=a_recv.at[layer, par, piece, src_col],
            device_id={"col": others[j]}, device_id_type=MESH)

    def gather_start(layer, piece, par):
        for j in range(3):
            gather(layer, piece, par, j, col).start()

    def gather_wait_send(layer, par):
        for piece in range(len(PIECES)):
            for j in range(3):
                gather(layer, piece, par, j, col).wait_send()

    def gather_wait(layer, par):
        for piece in range(len(PIECES)):
            for j in range(3):
                gather(layer, piece, par, j, others[j]).wait_recv()

    def columns(i, start, size):
        return pl.ds(pl.multiple_of(owners[i] * tile_step + start, LANES), size)

    whole = ((0, width),)

    def dot_block(layer, par, weights, i, parts):
        total = None
        for k in range(4):
            rhs = [weights[k * n:(k + 1) * n, columns(i, *part)] for part in parts]
            rhs = rhs[0] if len(rhs) == 1 else jnp.concatenate(rhs, axis=1)
            part_sum = jnp.dot(hblk[layer, par, k, :, :n], rhs, preferred_element_type=F32)
            total = part_sum if total is None else total + part_sum
        return total

    def send_sums(layer, par, product, other, between):
        def block(i, parts):
            z, at = product(i, parts), 0
            for start, size in parts:
                zb[layer, i, :, start:start + size] = z[:, at:at + size] + other(i, start, size)
                at += size

        sent = 0
        for strip in STRIPS:
            block(0, strip)
            for _ in strip:
                d2d(layer, par, sent).start()
                sent += 1
        got = 0
        for j, strip in enumerate(STRIPS):
            block(1, strip)
            for _ in strip:
                d2d(layer, par, got).wait_recv()
                got += 1
            at = slice(strip[0][0], min(sum(strip[0]), edge))
            zb[layer, 1, :, at] = zb[layer, 1, :, at] + rd[layer, par, 0, :, at]
            if j == len(STRIPS) - 1:
                pack_edges(layer, par)
            ysum(layer, par, j).start()
        yedge(layer, par, 0).start()
        for piece in range(1, len(PIECES)):
            ysum(layer, par, len(STRIPS) + piece - 1).start()
            yedge(layer, par, piece).start()
        block(2, whole)
        d2d(layer, par, len(D2D_LANES)).start()
        between()
        block(3, whole)

    def cell_update(layer, piece, par, step):
        if piece == 0:
            d2d(layer, par, len(D2D_LANES)).wait_recv()
            for j in range(len(STRIPS)):
                ysum(layer, par, j).wait_recv()
        else:
            ysum(layer, par, len(STRIPS) + piece - 1).wait_recv()
        yedge(layer, par, piece).wait_recv()
        unpack_edges(layer, piece, par)
        span = pad_n + LANES
        unit = lax.broadcasted_iota(jnp.int32, (ROW_CHUNK, pad_n), 1)
        start0 = row * (4 * n - tile_step)
        first, size = PIECES[piece]
        for q in range(first, first + size, ROW_CHUNK):
            rows = pl.ds(q, ROW_CHUNK)
            gates = []
            for m in range(4):
                start = start0 + m * n
                tile = jnp.minimum(start // LANES, (width - span) // LANES)
                shift = start - tile * LANES
                at = pl.ds(pl.multiple_of(tile * LANES, LANES), span)
                z = zb[layer, 3, rows, at] + rd[layer, par, 1, rows, at] + yr[layer, par, rows, at]
                z = pltpu.roll(z, span - shift, axis=1)[:, :pad_n]
                gates.append(z + bias[layer, m:m + 1, :])
            c_new = (jax.nn.sigmoid(gates[1]) * cell[layer, rows, :]
                     + jax.nn.sigmoid(gates[0]) * jnp.tanh(gates[2]))
            cell[layer, rows, :] = c_new
            h_new = jnp.where(unit < n, jax.nn.sigmoid(gates[3]) * jnp.tanh(c_new), 0.0).astype(BF16)
            hblk[layer, par, col, rows, :] = h_new
            if layer == 1:
                h2_out[step, rows, :] = h_new[:, :n]

    def wait_sum_sends(layer, par):
        for j in range(len(D2D_LANES) + 1):
            d2d(layer, par, j).wait_send()
        for j in range(y_copies):
            ysum(layer, par, j).wait_send()
        for piece in range(len(PIECES)):
            yedge(layer, par, piece).wait_send()

    def finish(layer, piece, par, step, first):
        if piece == 0:
            @pl.when(jnp.logical_not(first))
            def _():
                gather_wait_send(layer, 1 - par)

        cell_update(layer, piece, par, step)
        gather_start(layer, piece, par)
        if piece == len(PIECES) - 1:
            wait_sum_sends(layer, par)

    def step_body(s, carry):
        par = lax.rem(s, 2)
        prev = 1 - par

        def finish_two():
            @pl.when(s >= 2)
            def _():
                finish(1, 1, par, s - 2, s == 2)

        @pl.when(s > 0)
        def _():
            gather_wait(0, prev)

        @pl.when(s < steps)
        def _():
            pin_copy(s).wait()

            @pl.when(s + 1 < steps)
            def _():
                pin_copy(s + 1).start()

            @pl.when(s == 0)
            def _():
                w_copies[0].wait()

            send_sums(0, par, lambda i, parts: dot_block(0, prev, w1, i, parts),
                      lambda i, start, size: pin[par, :, columns(i, start, size)], finish_two)

        @pl.when(s == steps)
        def _():
            finish_two()

        @pl.when(s >= 2)
        def _():
            finish(1, 2, par, s - 2, s == 2)

        @pl.when(s == 1)
        def _():
            w_copies[1].wait()
            w_copies[2].wait()

        @pl.when(s >= 1)
        def _():
            for i in range(4):
                zb[1, i] = dot_block(0, prev, w2i, i, whole)

        @pl.when(s == 0)
        def _():
            run_project(1)

        @pl.when(s < steps)
        def _():
            finish(0, 0, par, s, s == 0)

        def finish_one():
            @pl.when(s < steps)
            def _():
                finish(0, 1, par, s, s == 0)

        @pl.when(s >= 1)
        def _():
            @pl.when(s >= 2)
            def _():
                gather_wait(1, par)

            send_sums(1, prev, lambda i, parts: dot_block(1, par, w2r, i, parts),
                      lambda i, start, size: zb[1, i, :, start:start + size], finish_one)

        @pl.when(s == 0)
        def _():
            run_project(2)
            finish_one()

        @pl.when(s < steps)
        def _():
            finish(0, 2, par, s, s == 0)

        @pl.when(s == 0)
        def _():
            run_project(3)
            w_copies[2].start()

        @pl.when(jnp.logical_and(s >= 1, s < steps))
        def _():
            finish(1, 0, prev, s - 1, s == 1)

        return carry

    lax.fori_loop(0, steps + 1, step_body, 0)

    last = (steps - 1) % 2
    gather_wait_send(1, 1 - last)
    gather_wait_send(0, last)
    for piece in range(len(PIECES)):
        cell_update(1, piece, last, steps - 1)
    wait_sum_sends(1, last)
    c1_out[...] = cell[0, :, :n]
    c2_out[...] = cell[1, :, :n]


def solution(mesh):
    def local_program(seq_in, w_in1, w_rec1, b_gate1, w_in2, w_rec2, b_gate2, h_init, c_init):
        steps, batch, rows_dev = seq_in.shape
        cols_dev = w_in1.shape[1]
        n = b_gate1.shape[0] // 4
        pad_n = -(-n // LANES) * LANES
        width = -(-rows_dev // LANES) * LANES

        h0 = h_init.astype(BF16).reshape(2, batch, 4, n).transpose(0, 2, 1, 3)
        c0 = lax.dynamic_slice_in_dim(c_init, lax.axis_index("col") * n, n, axis=2)
        biases = (b_gate1.reshape(4, n), b_gate2.reshape(4, n))

        def kernel(*refs):
            lstm_kernel(steps, batch, n, rows_dev, cols_dev, width, pad_n, *refs)

        hbm = pl.BlockSpec(memory_space=pl.ANY)
        vmem = pl.BlockSpec(memory_space=pltpu.VMEM)
        dma = pltpu.SemaphoreType.DMA
        hops, pieces = len(D2D_LANES) + 1, len(PIECES)
        sends = len(STRIPS) + pieces - 1
        return pl.pallas_call(
            kernel,
            name="lstm_grid",
            out_shape=(jax.ShapeDtypeStruct((steps, batch, n), BF16),
                       jax.ShapeDtypeStruct((batch, n), F32),
                       jax.ShapeDtypeStruct((batch, n), F32),
                       jax.ShapeDtypeStruct((steps, batch, cols_dev), F32)),
            in_specs=[hbm] * 5 + [vmem] * 4,
            out_specs=(vmem, vmem, vmem, hbm),
            scratch_shapes=[
                pltpu.VMEM((rows_dev, cols_dev), BF16),
                pltpu.VMEM((rows_dev, cols_dev), BF16),
                pltpu.VMEM((rows_dev, cols_dev), BF16),
                pltpu.VMEM((2, GROUP, batch, rows_dev), BF16),
                pltpu.VMEM((2, batch, cols_dev), F32),
                pltpu.VMEM((2, batch, pad_n), F32),
                pltpu.VMEM((2, 8, pad_n), F32),
                pltpu.VMEM((2, 2, 4, batch, pad_n), BF16),
                pltpu.VMEM((2, 4, batch, width), F32),
                pltpu.VMEM((2, 2, 2, batch, width), F32),
                pltpu.VMEM((2, 2, batch, width), F32),
                pltpu.VMEM((2, len(PIECES), ROW_CHUNK, LANES), F32),
                pltpu.VMEM((2, 2, len(PIECES), ROW_CHUNK, LANES), F32),
                dma((3,)), dma((4,)), dma((2,)), dma((2,)), dma((2,)),
                dma((2, hops)), dma((2, 2, hops)),
                dma((2, sends)), dma((2, 2, sends)),
                dma((2, pieces)), dma((2, 2, pieces)),
                dma((2, pieces, 3)), dma((2, 2, pieces, 4)),
            ],
            compiler_params=pltpu.CompilerParams(
                collective_id=0, has_side_effects=True, vmem_limit_bytes=67043328),
        )(seq_in, w_in1, w_rec1, w_in2, w_rec2, h0, c0, *biases)[:3]

    row_spec = P(None, "dp", "row")
    weight_spec = P("row", "col")
    bias_spec = P(("col", "row"))
    seq_out_spec = P(None, "dp", ("row", "col"))
    cell_out_spec = P("dp", ("row", "col"))
    return jax.shard_map(
        local_program,
        mesh=mesh,
        in_specs=(row_spec, weight_spec, weight_spec, bias_spec, weight_spec, weight_spec, bias_spec, row_spec, row_spec),
        out_specs=(seq_out_spec, cell_out_spec, cell_out_spec),
        check_vma=False,
    )
```

time: 352 us -> 335 us (0.952)
  matrix products: 25.7 us -> 0 us
  Pallas kernels: 314 us -> 322 us
    dot_general x1 -> x0, matrix products: 25.7 us -> none  [local_program(): jnp.dot(seq_in.reshape(steps * batch, rows_dev), w_in1, preferred_element...]
    pallas_call x1, Pallas kernels: 314 us -> 322 us  [local_program(): pl.pallas_call(kernel, name='lstm_grid', out_shape=(jax.ShapeDtypeStruct(...]
where the time goes in v3:
time: 335 us
  Pallas kernels  322 us (96%)
  local copies, waits for them, and re-layouts  10.9 us (3%)
    pallas_call x1, Pallas kernels, local_program(): pl.pallas_call(kernel, name='lstm_grid', out_shape=(jax.ShapeDtypeStruct(...  322 us

profile of v3, /device:TPU:0, one launch (start us, length us, event | category | flops | bytes accessed | tf_op | source)
XLA Modules:
  0.0 334.7 jit_solution(7059016329385772779)
XLA Ops:
  0.6 1.4 reshape.16.refs_7_
  2.0 1.4 reshape.17.refs_8_
  3.4 1.7 constant_dynamic-slice_fusion.refs_6_
  5.1 1.2 convert_element_type.3
  6.3 0.4 reshape.15
  6.7 0.8 copy.14
  7.5 322.0 %lstm_grid.1 = (bf16[16,64,360]{2,1,0:T(8,128)(2,1)}, f32[64,360]{1,0:T(8,128)}, f32[64,360]{1,0:T(8,128)}, f32[16,64,5760]{2,1,0:T(8,128)}) custom-call(bf16[16,64,1440]{2,1,0:T(8,128)(2,1)} %refs_0_.1, bf16[1440,5760]{1,0:T(8,128)(2,1)} %refs_1_.1, bf16[1440,5760]{1,0:T(8,128)(2,1)} %refs_2_.1, bf16[1440,5760]{1,0:T(8,128)(2,1)} %refs_3_.1, ...), custom_call_target="tpu_custom_call" | custom-call | tf_op jit(solution)/shard_map/lstm_grid/pallas_call | solution.py:410
  329.5 2.1 copy.18
  331.6 1.5 copy.19
  333.1 1.5 copy.20

commit v4 on v3

--- a/solution.py
+++ b/solution.py
@@ -96,11 +96,16 @@
         pl.semaphore_signal(barrier, inc=1, device_id={"col": lax.rem(col + j, 4)}, device_id_type=MESH)
 
     for layer in range(2):
-        hblk[layer, 1, :, :, :n] = h0_ref[layer]
         cell[layer] = jnp.zeros((batch, pad_n), F32)
-        cell[layer, :, :n] = c0_ref[layer]
         bias[layer] = jnp.zeros((8, pad_n), F32)
-        bias[layer, :4, :n] = (b1_ref, b2_ref)[layer][...]
+        for k in range(4):
+            own = slice(k * n, (k + 1) * n)
+            hblk[layer, 1, k, :, :n] = h0_ref[layer, :, own].astype(BF16)
+            bias[layer, k:k + 1, :n] = (b1_ref, b2_ref)[layer][:, own]
+
+            @pl.when(col == k)
+            def _(own=own, layer=layer):
+                cell[layer, :, :n] = c0_ref[layer, :, own]
     first_pair = project(0)
     for jj in range(spans // 2):
         w1i_copy(2 * jj).wait()
@@ -227,14 +232,17 @@
             if j == len(STRIPS) - 1:
                 pack_edges(layer, par)
             ysum(layer, par, j).start()
+            if j == 0:
+                between(0)
         yedge(layer, par, 0).start()
         for piece in range(1, len(PIECES)):
             ysum(layer, par, len(STRIPS) + piece - 1).start()
             yedge(layer, par, piece).start()
         block(2, whole)
         d2d(layer, par, len(D2D_LANES)).start()
-        between()
+        between(1)
         block(3, whole)
+        between(2)
 
     def cell_update(layer, piece, par, step):
         if piece == 0:
@@ -291,10 +299,15 @@
         par = lax.rem(s, 2)
         prev = 1 - par
 
-        def finish_two():
+        def finish_two(piece):
             @pl.when(s >= 2)
             def _():
-                finish(1, 1, par, s - 2, s == 2)
+                finish(1, piece, par, s - 2, s == 2)
+
+        def finish_one(piece):
+            @pl.when(s < steps)
+            def _():
+                finish(0, piece, par, s, s == 0)
 
         @pl.when(s > 0)
         def _():
@@ -302,26 +315,22 @@
 
         @pl.when(s < steps)
         def _():
+            @pl.when(s == 0)
+            def _():
+                w_copies[0].wait()
+
+            @pl.when(s + 1 < steps)
+            def _():
+                pin_copy(s + 1).start()
+
             pin_copy(s).wait()
-
-            @pl.when(s + 1 < steps)
-            def _():
-                pin_copy(s + 1).start()
-
-            @pl.when(s == 0)
-            def _():
-                w_copies[0].wait()
-
             send_sums(0, par, lambda i, parts: dot_block(0, prev, w1, i, parts),
                       lambda i, start, size: pin[par, :, columns(i, start, size)], finish_two)
 
         @pl.when(s == steps)
         def _():
-            finish_two()
-
-        @pl.when(s >= 2)
-        def _():
-            finish(1, 2, par, s - 2, s == 2)
+            for piece in range(len(PIECES)):
+                finish_two(piece)
 
         @pl.when(s == 1)
         def _():
@@ -333,21 +342,6 @@
             for i in range(4):
                 zb[1, i] = dot_block(0, prev, w2i, i, whole)
 
-        @pl.when(s == 0)
-        def _():
-            run_project(1)
-
-        @pl.when(s < steps)
-        def _():
-            finish(0, 0, par, s, s == 0)
-
-        def finish_one():
-            @pl.when(s < steps)
-            def _():
-                finish(0, 1, par, s, s == 0)
-
-        @pl.when(s >= 1)
-        def _():
             @pl.when(s >= 2)
             def _():
                 gather_wait(1, par)
@@ -357,21 +351,13 @@
 
         @pl.when(s == 0)
         def _():
+            run_project(1)
+            finish_one(0)
             run_project(2)
-            finish_one()
-
-        @pl.when(s < steps)
-        def _():
-            finish(0, 2, par, s, s == 0)
-
-        @pl.when(s == 0)
-        def _():
+            finish_one(1)
+            finish_one(2)
             run_project(3)
             w_copies[2].start()
-
-        @pl.when(jnp.logical_and(s >= 1, s < steps))
-        def _():
-            finish(1, 0, prev, s - 1, s == 1)
 
         return carry
 
@@ -394,10 +380,6 @@
         n = b_gate1.shape[0] // 4
         pad_n = -(-n // LANES) * LANES
         width = -(-rows_dev // LANES) * LANES
-
-        h0 = h_init.astype(BF16).reshape(2, batch, 4, n).transpose(0, 2, 1, 3)
-        c0 = lax.dynamic_slice_in_dim(c_init, lax.axis_index("col") * n, n, axis=2)
-        biases = (b_gate1.reshape(4, n), b_gate2.reshape(4, n))
 
         def kernel(*refs):
             lstm_kernel(steps, batch, n, rows_dev, cols_dev, width, pad_n, *refs)
@@ -438,7 +420,7 @@
             ],
             compiler_params=pltpu.CompilerParams(
                 collective_id=0, has_side_effects=True, vmem_limit_bytes=67043328),
-        )(seq_in, w_in1, w_rec1, w_in2, w_rec2, h0, c0, *biases)[:3]
+        )(seq_in, w_in1, w_rec1, w_in2, w_rec2, h_init, c_init, b_gate1[None], b_gate2[None])[:3]
 
     row_spec = P(None, "dp", "row")
     weight_spec = P("row", "col")

time: 335 us -> 332 us (level)
    reshape x4 -> x0, local copies, waits for them, and re-layouts: 3.95 us -> none  [the longest x2 2.74 us: local_program(): biases = (b_gate1.reshape(4, n), b_gate2.reshape(4, n))]
where the time goes in v4:
time: 332 us
  Pallas kernels  323 us (97%)
  local copies, waits for them, and re-layouts  7.76 us (2%)
    pallas_call x1, Pallas kernels, local_program(): pl.pallas_call(kernel, name='lstm_grid', out_shape=(jax.ShapeDtypeStruct(...  323 us

profile of v4, /device:TPU:0, one launch (start us, length us, event | category | flops | bytes accessed | tf_op | source)
XLA Modules:
  0.0 331.7 jit_solution(14168153757807729241)
XLA Ops:
  0.6 1.3 broadcast_in_dim.6.refs_7_
  1.9 1.3 broadcast_in_dim.7.refs_8_
  3.2 323.3 %lstm_grid.1 = (bf16[16,64,360]{2,1,0:T(8,128)(2,1)}, f32[64,360]{1,0:T(8,128)}, f32[64,360]{1,0:T(8,128)}, f32[16,64,5760]{2,1,0:T(8,128)}) custom-call(bf16[16,64,1440]{2,1,0:T(8,128)(2,1)} %refs_0_.1, bf16[1440,5760]{1,0:T(8,128)(2,1)} %refs_1_.1, bf16[1440,5760]{1,0:T(8,128)(2,1)} %refs_2_.1, bf16[1440,5760]{1,0:T(8,128)(2,1)} %refs_3_.1, ...), custom_call_target="tpu_custom_call" | custom-call | tf_op jit(solution)/shard_map/lstm_grid/pallas_call | solution.py:392
  326.5 2.1 copy.15
  328.6 1.5 copy.16
  330.2 1.5 copy.17
